TPU v7x, 512 devices: a 8x2x16 block of a 8x8x16 slice. The times are simulated.
512 devices in a mesh: grp: 2 (over y), tx: 16 (over z), ty: 16 (over x, core).
Axes of the slice: x: 8, y: 2, z: 16, core: 2. Of those that a mesh axis runs over, the one named last changes fastest.
The devices are a block of a 8x8x16 slice.
Arguments:
- obj_field: float32 [2, 4096, 2048], P(None, ('grp', 'tx'), 'ty'), parts along dimension 1, may hold values from -6 to 6
- eigenprobes: bfloat16 [2, 32, 128, 128], P(None, 'grp'), parts along dimension 1, may hold values from -1.5 to 1.5
- weights: float32 [32, 16, 3, 16], P(('grp', 'tx'), 'ty'), parts along dimension 0, may hold values from -4 to 4
- offsets: int32 [32, 16, 3, 2], P(('grp', 'tx'), 'ty'), parts along dimension 0, may hold values from 0 to 127
- counts: int32 [32, 16], P(('grp', 'tx'), 'ty'), parts along dimension 0, may hold values from 1 to 3, as said below
- amplitudes: bfloat16 [32, 16, 3, 128, 128], P(('grp', 'tx'), 'ty'), parts along dimension 0, may hold values from 0.19921875 to 3
Outputs:
- new_object: float32 [2, 4096, 2048], P(None, ('grp', 'tx'), 'ty'), parts along dimension 1
- new_eigenprobes: float32 [2, 32, 128, 128], P(None, 'grp'), parts along dimension 1
There are 2 independent parts, one for each index of `grp`. A program takes and returns all parts, laid end to end along the dimension named above; each array names one. Nothing has to cross between parts.
Inputs may be any that keep to these rules, and one draw needn't show every extreme that they name: Every tile holds 1 to 3 positions; some tile holds exactly 3; slots from counts on are unused.
All inputs are finite; a program needn't handle non-finite values.
Results may differ from a plain program's by a relative error of at most 0.0003.
Values sent between devices are 32-bit elements; how exact they have to be, the bound alone decides.
No kernel may reach another device: no remote copies, remote signals or barrier semaphores. Data moves between devices by JAX's collectives and lax.ppermute only.
A program may use at most 64 MiB of HBM per device.

v0:
```python
import functools
import math
import jax
import jax.numpy as jnp
from jax import lax
from jax.sharding import Mesh
from jax.sharding import PartitionSpec as P

TY = ("ty_0", "ty_1")
TX_TY = ("tx", "ty_0", "ty_1")
high = lax.Precision.HIGHEST


def from_behind(value, axis, steps):
    count = lax.axis_size(axis)
    pairs = [(source, (source + steps) % count) for source in range(count)]
    return lax.ppermute(value, axis, pairs)


def one_axis_at_a_time(shard, axes):
    return functools.reduce(lax.psum, axes, shard)


def in_blocks(shard, dim, count):
    before, after = (shard.shape[:dim], shard.shape[dim + 1 :])
    return jnp.moveaxis(shard.reshape(*before, count, -1, *after), dim, 0)


def sent_and_summed(shard, axis, dim):
    tiles = in_blocks(shard, dim, lax.axis_size(axis))
    arrived = lax.all_to_all(tiles, axis, split_axis=0, concat_axis=0, tiled=True)
    return arrived.sum(axis=0)


def gathered_total(shard, axis):
    return lax.all_gather(shard, axis).sum(0)


def tables(frame, sign):
    grid = jnp.arange(frame, dtype=jnp.int32)
    phase = grid[:, None] * grid[None, :] % frame
    angle = phase.astype(jnp.float32) * (2.0 * math.pi / frame)
    scale = 1.0 / math.sqrt(frame)
    return (jnp.cos(angle) * scale, sign * jnp.sin(angle) * scale)


def transform(real_part, imag_part, table_re, table_im):
    left_re = jnp.einsum("jk,skl->sjl", table_re, real_part, precision=high) - jnp.einsum(
        "jk,skl->sjl", table_im, imag_part, precision=high
    )
    left_im = jnp.einsum("jk,skl->sjl", table_re, imag_part, precision=high) + jnp.einsum(
        "jk,skl->sjl", table_im, real_part, precision=high
    )
    out_re = jnp.einsum("sjk,kl->sjl", left_re, table_re, precision=high) - jnp.einsum(
        "sjk,kl->sjl", left_im, table_im, precision=high
    )
    out_im = jnp.einsum("sjk,kl->sjl", left_re, table_im, precision=high) + jnp.einsum(
        "sjk,kl->sjl", left_im, table_re, precision=high
    )
    return (out_re, out_im)


def row_divisor(norms, start, count, frame, modes):
    mode_of_row = (start + jnp.arange(count, dtype=jnp.int32)) // frame % modes
    match = mode_of_row[:, None] == jnp.arange(modes, dtype=jnp.int32)[None, :]
    return jnp.sum(jnp.where(match, norms[None, :] + 1.0, 0.0), axis=1)


def per_device(obj_field, eigenprobes, weights, offsets, counts, amplitudes):
    tile = obj_field.shape[1]
    modes = eigenprobes.shape[1]
    frame = eigenprobes.shape[2]
    slots = weights.shape[2]
    wts = weights[0, 0]
    offs = offsets[0, 0]
    live = (jnp.arange(slots, dtype=jnp.int32) < counts[0, 0]).astype(jnp.float32)
    local_norms = jnp.sum(live[:, None] * wts * wts, axis=0)
    below = from_behind(obj_field, "tx", -1)
    tall = jnp.concatenate([obj_field, below], axis=1)
    beside = from_behind(tall, TY, -1)
    region = jnp.concatenate([tall, beside], axis=2)
    zero_index = jnp.int32(0)

    def read_window(row_start, col_start):
        return lax.dynamic_slice(region, (zero_index, row_start, col_start), (2, frame, frame))

    windows = jax.vmap(read_window)(offs[:, 0], offs[:, 1])
    win_re = windows[:, 0]
    win_im = windows[:, 1]
    eig32 = eigenprobes.astype(jnp.float32)
    probe = jnp.einsum("sk,ckij->csij", wts, eig32, precision=high)
    psi_re = probe[0] * win_re - probe[1] * win_im
    psi_im = probe[0] * win_im + probe[1] * win_re
    fwd_re, fwd_im = tables(frame, -1.0)
    spec_re, spec_im = transform(psi_re, psi_im, fwd_re, fwd_im)
    amps = amplitudes[0, 0].astype(jnp.float32)
    factor = (amps / jnp.sqrt(spec_re * spec_re + spec_im * spec_im + 0.25) - 1.0) * live[
        :, None, None
    ]
    inv_re, inv_im = tables(frame, 1.0)
    chi_re, chi_im = transform(spec_re * factor, spec_im * factor, inv_re, inv_im)
    obj_re = probe[0] * chi_re + probe[1] * chi_im
    obj_im = probe[0] * chi_im - probe[1] * chi_re
    power = (probe[0] * probe[0] + probe[1] * probe[1]) * live[:, None, None]
    pieces = jnp.stack([obj_re, obj_im, power], axis=1)

    def add_slot(slot, acc):
        row_start = offs[slot, 0]
        col_start = offs[slot, 1]
        piece = lax.dynamic_index_in_dim(pieces, slot, 0, keepdims=False)
        current = lax.dynamic_slice(acc, (zero_index, row_start, col_start), (3, frame, frame))
        return lax.dynamic_update_slice(acc, current + piece, (zero_index, row_start, col_start))

    acc = jnp.zeros((3, tile + frame, tile + frame), jnp.float32)
    acc = lax.fori_loop(0, slots, add_slot, acc)
    grad_re = win_re * chi_re + win_im * chi_im
    grad_im = win_re * chi_im - win_im * chi_re
    slot_grad = jnp.stack([grad_re, grad_im])
    spilled = from_behind(acc[:, :, tile:], TY, 1)
    merged = acc[:, :, :tile].at[:, :, :frame].add(spilled)
    dropped = from_behind(merged[:, tile:, :], "tx", 1)
    totals = merged[:, :tile, :].at[:, :frame, :].add(dropped)
    local_illum = jnp.sum(totals[2])
    norms, illum_sum = (
        one_axis_at_a_time(local_norms, TX_TY),
        one_axis_at_a_time(local_illum, TX_TY),
    )
    cells = lax.axis_size("tx") * lax.axis_size(TY) * tile * tile
    mean_illum = illum_sum / cells
    new_object = obj_field + totals[:2] / (totals[2] + mean_illum)[None]
    flat_rows = 2 * modes * frame
    flat_eig = eig32.reshape(flat_rows, frame)
    gprobe = jnp.einsum("sk,csij->ckij", wts, slot_grad, precision=high)
    flat_grad = gprobe.reshape(flat_rows, frame)
    share_rows = flat_rows // lax.axis_size("tx")
    start = lax.axis_index("tx") * share_rows
    partial_value = sent_and_summed(flat_grad, "tx", 0)
    share = gathered_total(partial_value, TY)
    own = lax.dynamic_slice_in_dim(flat_eig, start, share_rows, 0)
    updated = own + share / row_divisor(norms, start, share_rows, frame, modes)[:, None]
    new_eig = lax.all_gather(updated, "tx", axis=0, tiled=True).reshape(2, modes, frame, frame)
    return (new_object, new_eig)


def solution(mesh):
    finer = Mesh(
        mesh.devices.reshape(mesh.shape["grp"], mesh.shape["tx"], 8, 2),
        ("grp", "tx", "ty_0", "ty_1"),
    )
    return jax.shard_map(
        per_device,
        mesh=finer,
        in_specs=(
            P(None, ("grp", "tx"), TY),
            P(None, "grp", None, None),
            P(("grp", "tx"), TY, None, None),
            P(("grp", "tx"), TY, None, None),
            P(("grp", "tx"), TY),
            P(("grp", "tx"), TY, None, None, None),
        ),
        out_specs=(P(None, ("grp", "tx"), TY), P(None, "grp", None, None)),
        check_vma=False,
    )
```

profile of v0, /device:TPU:66, one launch (start us, length us, event | category | flops | bytes accessed | tf_op | source)
XLA Modules:
  0.0 368.5 jit_solution(7381467266140601053)
XLA Ops:
  7.2 44.0 %collective-permute-start = (f32[2,128,128]{2,1,0:T(8,128)}, f32[2,128,128]{2,1,0:T(8,128)S(1)}, u32[]{:S(2)}, u32[]{:S(2)}) collective-permute-start(f32[2,128,128]{2,1,0:T(8,128)} %param.16), channel_id=1, source_target_pairs={{0,240},{16,0},{32,16},{48,32},{64,48},{80,64},{96,80},{112,96},{1... | collective-permute-start | bytes 393224 | tf_op jit(solution)/shard_map/ppermute | solution.py:17
  51.9 0.8 compare_select_fusion.1
  52.8 0.9 constant_dynamic-update-slice_fusion.1
  54.5 2.2 convolution_bitcast_fusion.1
  56.7 1.7 collective-permute-done.1
  58.4 15.2 %while.19 = (s32[]{:T(128)}, f32[2,256,256]{2,1,0:T(8,128)S(1)}, s32[3,3]{1,0:T(4,128)S(1)}, f32[3,2,128,128]{3,0,2,1:T(4,128)S(1)}, s32[]{:T(128)}, /*index=5*/s32[]{:T(128)}) while((s32[]{:T(128)}, f32[2,256,256]{2,1,0:T(8,128)S(1)}, s32[3,3]{1,0:T(4,128)S(1)}, f32[3,2,128,128]{3,0,2,1:T(4,128)S(1)}, s32[]{:T(128)}, /*index=5*/s32[]{:T(128)}) %tuple.75), condition=%wide.while_cond.2, body=%wide.while_body.2.sunk | while | flops 2 | bytes 524421 | solution.py:85
  59.0 1.3 constant_dynamic-slice_fusion.12
  60.3 3.1 dynamic-update-slice.11
  64.0 1.3 constant_dynamic-slice_fusion.12
  65.3 3.1 dynamic-update-slice.11
  69.0 1.3 constant_dynamic-slice_fusion.12
  70.3 3.1 dynamic-update-slice.11
  80.5 0.8 fusion
  82.5 0.8 fusion.1
  85.3 2.1 convolution_bitcast_fusion
  88.0 98.6 %all_to_all.5 = f32[16,256,128]{2,1,0:T(8,128)S(1)} all-to-all(f32[16,256,128]{2,1,0:T(8,128)S(1)} %bitcast.175), channel_id=1, replica_groups=mesh['grp'=2,'tx'=16,'ty_0'=8,'ty_1'=2] {'tx'}, dimensions={0} | all-to-all | bytes 4194304 | tf_op jit(solution)/shard_map/all_to_all | solution.py:31
  186.6 0.8 reduce_sum.46
  188.0 22.8 %while.18 = (s32[]{:T(128)}, f32[3,256,256]{2,1,0:T(8,128)S(1)}, s32[3,2]{0,1:T(2,128)S(1)}, f32[3,3,128,128]{3,0,2,1:T(4,128)S(1)}, s32[]{:T(128)}, /*index=5*/s32[]{:T(128)}, s32[]{:T(128)}) while((s32[]{:T(128)}, f32[3,256,256]{2,1,0:T(8,128)S(1)}, s32[3,2]{0,1:T(2,128)S(1)}, f32[3,3,128,128]{3,0,2,1:T(4,128)S(1)}, s32[]{:T(128)}, ...), condition=%wide.region_1.2_spmd, body=%wide.region_0.0_spmd.sunk | while | flops 49160 | bytes 1376445 | solution.py:115
  192.7 2.9 dynamic_update_slice.8
  200.2 2.9 dynamic_update_slice.8
  207.8 3.0 dynamic_update_slice.8
  210.9 3.6 collective-permute-start.2
  214.4 6.8 %collective-permute-done.2 = f32[3,256,128]{2,1,0:T(8,128)S(1)} collective-permute-done((f32[3,256,128]{2,1,0:T(8,128)S(1)}, f32[3,256,128]{2,1,0:T(8,128)S(1)}, u32[]{:S(2)}, u32[]{:S(2)}) %collective-permute-start.2) | collective-permute-done | bytes 393248 | tf_op jit(solution)/shard_map/ppermute | solution.py:17
  221.3 3.6 collective-permute-start.3
  225.1 5.6 %collective-permute-done.3 = f32[3,128,128]{2,1,0:T(8,128)S(1)} collective-permute-done((f32[3,128,128]{2,1,0:T(8,128)S(1)}, f32[3,128,128]{2,1,0:T(8,128)S(1)}, u32[]{:S(2)}, u32[]{:S(2)}) %collective-permute-start.3) | collective-permute-done | bytes 196640 | tf_op jit(solution)/shard_map/ppermute | solution.py:17
  231.4 31.6 %all-reduce = (f32[]{:T(128)}, f32[16]{0:T(128)S(1)}) all-reduce(f32[]{:T(128)} %slice_reduce_fusion, f32[16]{0:T(128)S(1)} %fusion.80), channel_id=1, replica_groups=mesh['grp'=2,'tx'=16,'ty_0'=8,'ty_1'=2] {'tx'}, use_global_device_ids=true, to_apply=%region_3.4 | all-reduce | flops 17 | bytes 136 | tf_op jit(solution)/shard_map/psum | solution.py:21
  263.0 20.4 %all-reduce.1 = (f32[]{:T(128)}, f32[16]{0:T(128)S(1)}) all-reduce(f32[]{:T(128)} %get-tuple-element.170, f32[16]{0:T(128)S(1)} %get-tuple-element.171), channel_id=1, replica_groups=mesh['grp'=2,'tx'=16,'ty_0'=8,'ty_1'=2] {'ty_0'}, use_global_device_ids=true, to_apply=%region_4.5 | all-reduce | flops 17 | bytes 136 | tf_op jit(solution)/shard_map/psum | solution.py:21
  283.4 3.1 all-reduce.2
  286.7 1.7 reduce_sum.47
  288.4 1.6 convert_add_fusion
  291.3 67.1 %all-gather.4.cloned.1.call-done = f32[4096,128]{1,0:T(8,128)} async-done(((f32[256,128]{1,0:T(8,128)}), f32[4096,128]{1,0:T(8,128)}) %all-gather.4.cloned.1.call-update) | async-done | bytes 2097168 | tf_op jit(solution)/shard_map/all_gather | solution.py:141
  358.5 3.1 copy.171
  (70 shorter events, 18.4 us)
Async XLA Ops:
  7.2 279.5 %all-gather.6.cloned.1.call-start = ((), (), s32[]{:S(2)}) async-start(), calls=%async_computation.2 | async-start | bytes 2228224 | tf_op jit(solution)/shard_map/all_gather | solution.py:36
  7.2 47.1 %collective-permute-start = (f32[2,128,128]{2,1,0:T(8,128)}, f32[2,128,128]{2,1,0:T(8,128)S(1)}, u32[]{:S(2)}, u32[]{:S(2)}) collective-permute-start(f32[2,128,128]{2,1,0:T(8,128)} %param.16), channel_id=1, source_target_pairs={{0,240},{16,0},{32,16},{48,32},{64,48},{80,64},{96,80},{112,96},{1... | collective-permute-start | bytes 393224 | tf_op jit(solution)/shard_map/ppermute | solution.py:17
  54.4 4.0 %collective-permute-start.1 = (f32[2,256,128]{2,1,0:T(8,128)S(1)}, f32[2,256,128]{2,1,0:T(8,128)S(1)}, u32[]{:S(2)}, u32[]{:S(2)}) collective-permute-start(f32[2,256,128]{2,1,0:T(8,128)S(1)} %constant_dynamic-update-slice_fusion), channel_id=1, source_target_pairs={{0,15},{1,0},{2,1},{3,2},{4,3},{5,4},{6,5},{7,6},{8,7},{9,8},{10,9... | collective-permute-start | bytes 786440 | tf_op jit(solution)/shard_map/ppermute | solution.py:17
  74.4 4.5 %copy-start.1 = (bf16[1,1,3,128,128]{4,3,2,1,0:T(8,128)(2,1)S(1)}, bf16[1,1,3,128,128]{4,3,2,1,0:T(8,128)(2,1)}, u32[]{:S(2)}) copy-start(bf16[1,1,3,128,128]{4,3,2,1,0:T(8,128)(2,1)} %param.21) | copy-start | bytes 294916
  82.5 2.7 copy-start.3
  187.4 0.7 copy-start.2
  187.4 171.0 %all-gather.4.cloned.1.call-start = ((), (), s32[]{:S(2)}) async-start(), calls=%async_computation.1 | async-start | bytes 2228224 | tf_op jit(solution)/shard_map/all_gather | solution.py:141
  210.9 10.4 %collective-permute-start.2 = (f32[3,256,128]{2,1,0:T(8,128)S(1)}, f32[3,256,128]{2,1,0:T(8,128)S(1)}, u32[]{:S(2)}, u32[]{:S(2)}) collective-permute-start(f32[3,256,128]{2,1,0:T(8,128)S(1)} %slice.92), channel_id=1, source_target_pairs={{0,1},{1,2},{2,3},{3,4},{4,5},{5,6},{6,7},{7,8},{8,9},{9,10},{10,1... | collective-permute-start | bytes 1179656 | tf_op jit(solution)/shard_map/ppermute | solution.py:17
  221.3 69.4 %copy-start = (f32[2,128,128]{2,1,0:T(8,128)S(1)}, f32[2,128,128]{2,1,0:T(8,128)}, u32[]{:S(2)}) copy-start(f32[2,128,128]{2,1,0:T(8,128)} %param.16) | copy-start | bytes 393220
  221.3 9.4 %collective-permute-start.3 = (f32[3,128,128]{2,1,0:T(8,128)S(1)}, f32[3,128,128]{2,1,0:T(8,128)S(1)}, u32[]{:S(2)}, u32[]{:S(2)}) collective-permute-start(f32[3,128,128]{2,1,0:T(8,128)S(1)} %slice.115), channel_id=1, source_target_pairs={{0,16},{16,32},{32,48},{48,64},{64,80},{80,96},{96,112},{112,128},... | collective-permute-start | bytes 589832 | tf_op jit(solution)/shard_map/ppermute | solution.py:17
Sparse Core Ops, SparseCore 0:
  187.5 45.9 all-gather.5
  290.2 68.2 all-gather.3
where the time goes:
time: 369 us; the launch traced here: 368 us
  blocking collectives  154 us (42%)
  waiting for transfers between devices  82 us (22%)
  starting transfers between devices  51.5 us (14%)
  local copies, waits for them, and re-layouts  31.5 us (9%)
  between operations  15.7 us (4%)
  matrix products  14.7 us (4%)
  loops' own time  11.4 us (3%)
  other arithmetic  7.88 us (2%)
    all_to_all x1, blocking collectives, sent_and_summed(): lax.all_to_all(tiles, axis, split_axis=0, concat_axis=0, tiled=True)  98.6 us
    all_gather x1, waiting for transfers between devices, per_device(): lax.all_gather(updated, 'tx', axis=0, tiled=True)  67.1 us
    psum x3, blocking collectives, one_axis_at_a_time(): return functools.reduce(lax.psum, axes, shard)  55.2 us
    ppermute x4, starting transfers between devices, from_behind(): return lax.ppermute(value, axis, pairs)  51.3 us
    gather x12, local copies, waits for them, and re-layouts  14.9 us
    ppermute x4, waiting for transfers between devices, from_behind(): return lax.ppermute(value, axis, pairs)  14.8 us
    another operation x1, loops' own time, per_device(): acc = lax.fori_loop(0, slots, add_slot, acc)  11.1 us
    dynamic_update_slice x3, local copies, waits for them, and re-layouts, add_slot(): lax.dynamic_update_slice(acc, current + piece, (zero_index, row_start, co...  8.83 us
  transfers between devices with their start and end apart: 6, of which 5 were waited for; matrix products, arithmetic and copies ran while one was open for 5% of the time, Pallas kernels for 0%

commit v1 on v0

--- a/solution.py
+++ b/solution.py
@@ -67,6 +67,16 @@
 
 
 def per_device(obj_field, eigenprobes, weights, offsets, counts, amplitudes):
+
+    def carry_the_sources_all(message, dev_axis):
+        n = lax.axis_size(dev_axis)
+        log = tuple((n if ii == 0 else 1 for ii in range(message.ndim)))
+        row_out = jnp.tile(message, log)
+        w_next = lax.all_to_all(
+            row_out, axis_name=dev_axis, split_axis=0, concat_axis=0, tiled=True
+        )
+        return w_next
+
     tile = obj_field.shape[1]
     modes = eigenprobes.shape[1]
     frame = eigenprobes.shape[2]
@@ -138,7 +148,7 @@
     share = gathered_total(partial_value, TY)
     own = lax.dynamic_slice_in_dim(flat_eig, start, share_rows, 0)
     updated = own + share / row_divisor(norms, start, share_rows, frame, modes)[:, None]
-    new_eig = lax.all_gather(updated, "tx", axis=0, tiled=True).reshape(2, modes, frame, frame)
+    new_eig = carry_the_sources_all(updated, dev_axis="tx").reshape(2, modes, frame, frame)
     return (new_object, new_eig)
 
 

time: 369 us -> 401 us (1.087)
  the two profiles are of different devices: /device:TPU:66 before, /device:TPU:80 now
where the time goes in v1:
time: 401 us; the launch traced here: 400 us
  blocking collectives  149 us (37%)
  waiting for transfers between devices  115 us (29%)
  starting transfers between devices  55.9 us (14%)
  local copies, waits for them, and re-layouts  31.7 us (8%)
  between operations  15.7 us (4%)
  matrix products  14.7 us (4%)
  loops' own time  11.4 us (3%)
  other arithmetic  7.22 us (2%)
    all_to_all x1, blocking collectives, sent_and_summed(): lax.all_to_all(tiles, axis, split_axis=0, concat_axis=0, tiled=True)  101 us
    all_to_all x1, waiting for transfers between devices, carry_the_sources_all(): lax.all_to_all(row_out, axis_name=dev_axis, split_axis=0, concat_axis=0,...  93.6 us
    ppermute x4, starting transfers between devices, from_behind(): return lax.ppermute(value, axis, pairs)  50 us
    psum x3, blocking collectives, one_axis_at_a_time(): return functools.reduce(lax.psum, axes, shard)  48.1 us
    ppermute x4, waiting for transfers between devices, from_behind(): return lax.ppermute(value, axis, pairs)  21 us
    gather x12, local copies, waits for them, and re-layouts  15.5 us
    another operation x1, loops' own time, per_device(): acc = lax.fori_loop(0, slots, add_slot, acc)  11.1 us
    dynamic_update_slice x3, local copies, waits for them, and re-layouts, add_slot(): lax.dynamic_update_slice(acc, current + piece, (zero_index, row_start, co...  8.6 us
  transfers between devices with their start and end apart: 6, of which 5 were waited for; matrix products, arithmetic and copies ran while one was open for 4% of the time, Pallas kernels for 0%

profile of v1, /device:TPU:80, one launch (start us, length us, event | category | flops | bytes accessed | tf_op | source)
XLA Modules:
  0.0 400.1 jit_solution(12546892815534305653)
XLA Ops:
  7.2 44.0 %collective-permute-start = (f32[2,128,128]{2,1,0:T(8,128)}, f32[2,128,128]{2,1,0:T(8,128)S(1)}, u32[]{:S(2)}, u32[]{:S(2)}) collective-permute-start(f32[2,128,128]{2,1,0:T(8,128)} %param.16), channel_id=1, source_target_pairs={{0,240},{16,0},{32,16},{48,32},{64,48},{80,64},{96,80},{112,96},{1... | collective-permute-start | bytes 393224 | tf_op jit(solution)/shard_map/ppermute | solution.py:17
  51.9 0.8 compare_select_fusion.1
  52.8 0.9 constant_dynamic-update-slice_fusion.1
  54.4 2.5 collective-permute-start.1
  56.9 2.2 convolution_bitcast_fusion.1
  59.1 1.7 collective-permute-done.1
  60.9 15.8 %while.19 = (s32[]{:T(128)}, f32[2,256,256]{2,1,0:T(8,128)S(1)}, s32[3,3]{1,0:T(4,128)S(1)}, f32[3,2,128,128]{3,0,2,1:T(4,128)S(1)}, s32[]{:T(128)}, /*index=5*/s32[]{:T(128)}) while((s32[]{:T(128)}, f32[2,256,256]{2,1,0:T(8,128)S(1)}, s32[3,3]{1,0:T(4,128)S(1)}, f32[3,2,128,128]{3,0,2,1:T(4,128)S(1)}, s32[]{:T(128)}, /*index=5*/s32[]{:T(128)}) %tuple.75), condition=%wide.while_cond.2, body=%wide.while_body.2.sunk | while | flops 2 | bytes 524421 | solution.py:95
  61.6 1.4 constant_dynamic-slice_fusion.12
  63.0 3.1 dynamic-update-slice.11
  66.8 1.4 constant_dynamic-slice_fusion.12
  68.2 3.1 dynamic-update-slice.11
  72.0 1.4 constant_dynamic-slice_fusion.12
  73.4 3.1 dynamic-update-slice.11
  88.4 2.1 convolution_bitcast_fusion
  91.1 100.8 %all_to_all.11 = f32[16,256,128]{2,1,0:T(8,128)S(1)} all-to-all(f32[16,256,128]{2,1,0:T(8,128)S(1)} %bitcast.176), channel_id=1, replica_groups=mesh['grp'=2,'tx'=16,'ty_0'=8,'ty_1'=2] {'tx'}, dimensions={0} | all-to-all | bytes 4194304 | tf_op jit(solution)/shard_map/all_to_all | solution.py:31
  191.9 0.8 reduce_sum.46
  193.3 22.5 %while.18 = (s32[]{:T(128)}, f32[3,256,256]{2,1,0:T(8,128)S(1)}, s32[3,2]{0,1:T(2,128)S(1)}, f32[3,3,128,128]{3,0,2,1:T(4,128)S(1)}, s32[]{:T(128)}, /*index=5*/s32[]{:T(128)}, s32[]{:T(128)}) while((s32[]{:T(128)}, f32[3,256,256]{2,1,0:T(8,128)S(1)}, s32[3,2]{0,1:T(2,128)S(1)}, f32[3,3,128,128]{3,0,2,1:T(4,128)S(1)}, s32[]{:T(128)}, ...), condition=%wide.region_1.2_spmd, body=%wide.region_0.0_spmd.sunk | while | flops 49160 | bytes 1376445 | solution.py:125
  197.9 2.8 dynamic_update_slice.8
  205.4 3.0 dynamic_update_slice.8
  213.1 2.8 dynamic_update_slice.8
  216.0 11.6 %collective-permute-done.2 = f32[3,256,128]{2,1,0:T(8,128)S(1)} collective-permute-done((f32[3,256,128]{2,1,0:T(8,128)S(1)}, f32[3,256,128]{2,1,0:T(8,128)S(1)}, u32[]{:S(2)}, u32[]{:S(2)}) %collective-permute-start.2) | collective-permute-done | bytes 393248 | tf_op jit(solution)/shard_map/ppermute | solution.py:17
  227.6 3.4 collective-permute-start.3
  231.1 7.1 %collective-permute-done.3 = f32[3,128,128]{2,1,0:T(8,128)S(1)} collective-permute-done((f32[3,128,128]{2,1,0:T(8,128)S(1)}, f32[3,128,128]{2,1,0:T(8,128)S(1)}, u32[]{:S(2)}, u32[]{:S(2)}) %collective-permute-start.3) | collective-permute-done | bytes 196640 | tf_op jit(solution)/shard_map/ppermute | solution.py:17
  238.8 29.7 %all-reduce = (f32[]{:T(128)}, f32[16]{0:T(128)S(1)}) all-reduce(f32[]{:T(128)} %slice_reduce_fusion, f32[16]{0:T(128)S(1)} %fusion.80), channel_id=1, replica_groups=mesh['grp'=2,'tx'=16,'ty_0'=8,'ty_1'=2] {'tx'}, use_global_device_ids=true, to_apply=%region_3.4 | all-reduce | flops 17 | bytes 136 | tf_op jit(solution)/shard_map/psum | solution.py:21
  268.4 15.3 %all-reduce.1 = (f32[]{:T(128)}, f32[16]{0:T(128)S(1)}) all-reduce(f32[]{:T(128)} %get-tuple-element.170, f32[16]{0:T(128)S(1)} %get-tuple-element.171), channel_id=1, replica_groups=mesh['grp'=2,'tx'=16,'ty_0'=8,'ty_1'=2] {'ty_0'}, use_global_device_ids=true, to_apply=%region_4.5 | all-reduce | flops 17 | bytes 136 | tf_op jit(solution)/shard_map/psum | solution.py:21
  283.8 3.1 all-reduce.2
  287.0 1.7 reduce_sum.47
  288.7 1.0 convert_add_fusion
  289.7 1.5 tile.2
  291.2 5.8 %all-to-all-start.1 = ((f32[16,256,128]{2,1,0:T(8,128)}), f32[16,256,128]{2,1,0:T(8,128)S(1)}, u32[]{:S(2)}, u32[]{:S(2)}) async-start(f32[16,256,128]{2,1,0:T(8,128)} %tile.2), calls=%async_computation.1 | async-start | bytes 4194304 | tf_op jit(solution)/shard_map/all_to_all | solution.py:75
  298.4 93.6 %all-to-all-done.1 = f32[16,256,128]{2,1,0:T(8,128)S(1)} async-done(((f32[16,256,128]{2,1,0:T(8,128)}), f32[16,256,128]{2,1,0:T(8,128)S(1)}, u32[]{:S(2)}, u32[]{:S(2)}) %all-to-all-start.1) | async-done | bytes 2097184 | tf_op jit(solution)/shard_map/all_to_all | solution.py:75
  391.9 1.3 copy.171
  (70 shorter events, 20.2 us)
Async XLA Ops:
  7.2 279.8 %all-gather.3.cloned.1.call-start = ((), (), s32[]{:S(2)}) async-start(), calls=%async_computation.2 | async-start | bytes 2228224 | tf_op jit(solution)/shard_map/all_gather | solution.py:36
  7.2 47.1 %collective-permute-start = (f32[2,128,128]{2,1,0:T(8,128)}, f32[2,128,128]{2,1,0:T(8,128)S(1)}, u32[]{:S(2)}, u32[]{:S(2)}) collective-permute-start(f32[2,128,128]{2,1,0:T(8,128)} %param.16), channel_id=1, source_target_pairs={{0,240},{16,0},{32,16},{48,32},{64,48},{80,64},{96,80},{112,96},{1... | collective-permute-start | bytes 393224 | tf_op jit(solution)/shard_map/ppermute | solution.py:17
  54.4 6.4 %collective-permute-start.1 = (f32[2,256,128]{2,1,0:T(8,128)S(1)}, f32[2,256,128]{2,1,0:T(8,128)S(1)}, u32[]{:S(2)}, u32[]{:S(2)}) collective-permute-start(f32[2,256,128]{2,1,0:T(8,128)S(1)} %constant_dynamic-update-slice_fusion), channel_id=1, source_target_pairs={{0,15},{1,0},{2,1},{3,2},{4,3},{5,4},{6,5},{7,6},{8,7},{9,8},{10,9... | collective-permute-start | bytes 786440 | tf_op jit(solution)/shard_map/ppermute | solution.py:17
  77.5 4.5 %copy-start.1 = (bf16[1,1,3,128,128]{4,3,2,1,0:T(8,128)(2,1)S(1)}, bf16[1,1,3,128,128]{4,3,2,1,0:T(8,128)(2,1)}, u32[]{:S(2)}) copy-start(bf16[1,1,3,128,128]{4,3,2,1,0:T(8,128)(2,1)} %param.21) | copy-start | bytes 294916
  85.6 2.7 copy-start.3
  192.6 0.7 copy-start.2
  215.9 11.7 %collective-permute-start.2 = (f32[3,256,128]{2,1,0:T(8,128)S(1)}, f32[3,256,128]{2,1,0:T(8,128)S(1)}, u32[]{:S(2)}, u32[]{:S(2)}) collective-permute-start(f32[3,256,128]{2,1,0:T(8,128)S(1)} %slice.92), channel_id=1, source_target_pairs={{0,1},{1,2},{2,3},{3,4},{4,5},{5,6},{6,7},{7,8},{8,9},{9,10},{10,1... | collective-permute-start | bytes 1179656 | tf_op jit(solution)/shard_map/ppermute | solution.py:17
  227.6 10.5 %collective-permute-start.3 = (f32[3,128,128]{2,1,0:T(8,128)S(1)}, f32[3,128,128]{2,1,0:T(8,128)S(1)}, u32[]{:S(2)}, u32[]{:S(2)}) collective-permute-start(f32[3,128,128]{2,1,0:T(8,128)S(1)} %slice.115), channel_id=1, source_target_pairs={{0,16},{16,32},{32,48},{48,64},{64,80},{80,96},{96,112},{112,128},... | collective-permute-start | bytes 589832 | tf_op jit(solution)/shard_map/ppermute | solution.py:17
  291.2 6.5 %copy-start = (f32[2,128,128]{2,1,0:T(8,128)S(1)}, f32[2,128,128]{2,1,0:T(8,128)}, u32[]{:S(2)}) copy-start(f32[2,128,128]{2,1,0:T(8,128)} %param.16) | copy-start | bytes 393220
  291.2 100.8 %all-to-all-start.1 = ((f32[16,256,128]{2,1,0:T(8,128)}), f32[16,256,128]{2,1,0:T(8,128)S(1)}, u32[]{:S(2)}, u32[]{:S(2)}) async-start(f32[16,256,128]{2,1,0:T(8,128)} %tile.2), calls=%async_computation.1 | async-start | bytes 4194304 | tf_op jit(solution)/shard_map/all_to_all | solution.py:75
Sparse Core Ops, SparseCore 0:
  192.8 40.1 all-gather.2
